TPU v7x, 512 devices: a 4x2x32 block of a 4x8x32 slice. The times are simulated.
512 devices in a mesh: groups: 2 (over y), cells: 128 (over z, x), side: 2 (over core).
Axes of the slice: x: 4, y: 2, z: 32, core: 2. Of those that a mesh axis runs over, the one named last changes fastest.
The devices are a block of a 4x8x32 slice.
Arguments:
- datasets: float32 [2, 2000, 131072], P('side', None, ('groups', 'cells')), parts along dimension 2, may hold values from -6 to 6
- sketch: float32 [64, 131072], P(None, ('groups', 'cells')), parts along dimension 1, may hold values from -6 to 6
Outputs:
- factors: float32 [2, 64, 131072], P('side', None, ('groups', 'cells')), parts along dimension 2
There are 2 independent parts, one for each index of `groups`. A program takes and returns all parts, laid end to end along the dimension named above; each array names one. Nothing has to cross between parts.
All inputs are finite; a program needn't handle non-finite values.
Results may differ from a plain program's by a relative error of at most 0.00009.
Values sent between devices are 32-bit elements; how exact they have to be, the bound alone decides.
No kernel may reach another device: no remote copies, remote signals or barrier semaphores. Data moves between devices by JAX's collectives and lax.ppermute only.
A program may use at most 64 MiB of HBM per device.

v0:
```python
import jax
import jax.numpy as jnp
from jax import lax
from jax.sharding import Mesh
from jax.sharding import PartitionSpec as P

CELLS = ("cells_0", "cells_1")
GROUPS_CELLS = ("groups", "cells_0", "cells_1")


def rows_for(lines, peers):
    spare = -len(lines) % peers
    return jnp.pad(lines, [(0, spare)] + [(0, 0)] * (lines.ndim - 1))


def sent_to_all(x, axis):
    peers = lax.axis_size(axis)
    return lax.all_to_all(jnp.broadcast_to(x[None], (peers, *x.shape)), axis, 0, 0, tiled=True)


def in_order(blocks, dim):
    shape = list(blocks.shape[1:])
    shape[dim] *= blocks.shape[0]
    return jnp.moveaxis(blocks, 0, dim).reshape(shape)


def gather_axes(x, axes, dim):
    far, near = axes
    initial = sent_to_all(x, far)
    blocks = jnp.swapaxes(sent_to_all(initial, near), 0, 1)
    return in_order(blocks.reshape(-1, *x.shape), dim)


def split_up(x, dim, peers):
    shape = x.shape
    blocks = x.reshape(*shape[:dim], peers, shape[dim] // peers, *shape[dim + 1 :])
    return jnp.moveaxis(blocks, dim, 0)


def sent_and_summed(x, axis, dim):
    peers = lax.axis_size(axis)
    blocks = lax.all_to_all(split_up(x, dim, peers), axis, 0, 0, tiled=True)
    return jnp.sum(blocks, axis=0)


def sum_in_two_steps(x, axes, dim):
    far, near = axes
    own = sent_and_summed(split_up(x, dim, lax.axis_size(far)), near, dim + 1)
    return jnp.sum(lax.all_to_all(own, far, 0, 0, tiled=True), axis=0)


def nested_sum(x, axes):
    lines = x.reshape(-1)
    padded = rows_for(lines, lax.axis_size(axes[0]) * lax.axis_size(axes[1]))
    whole = gather_axes(sum_in_two_steps(padded, axes, 0), axes, 0)
    return lax.slice_in_dim(whole, 0, len(lines)).reshape(x.shape)


def from_behind(value, axis, steps):
    count = lax.axis_size(axis)
    initial, last = (max(0, -steps), min(count, count - steps))
    return lax.ppermute(value, axis, [(source, source + steps) for source in range(initial, last)])


def nested_sum_2(x, axes):
    own = sum_in_two_steps(rows_for(x, lax.axis_size(axes[0]) * lax.axis_size(axes[1])), axes, 0)
    whole = gather_axes(own, axes, 0)
    return whole[: len(x)].reshape(x.shape)


def packed_total(arrays, axis):
    ends = [0]
    for a in arrays:
        ends.append(ends[-1] + a.size)
    running = nested_sum_2(jnp.concatenate([a.ravel() for a in arrays]), axis)
    return tuple((running[b:e].reshape(a.shape) for a, b, e in zip(arrays, ends, ends[1:])))


def per_device(datasets, sketch):
    high = lax.Precision.HIGHEST
    own_data = datasets[0]
    side_index = lax.axis_index("side")
    cell_count = own_data.shape[1] * lax.axis_size(CELLS)
    scale = jnp.sqrt(jnp.float32(cell_count))
    partial_value = jnp.dot(sketch, own_data.T, precision=high)
    summed = nested_sum(partial_value, ("cells_0", "cells_1"))
    arrived = from_behind(summed, "side", -1)
    panel = jnp.where(side_index == 0, arrived, summed)
    range_rows = jnp.dot(panel, own_data, precision=high)
    gram_part = jnp.dot(range_rows, range_rows.T, precision=high)
    raw_part = jnp.dot(range_rows, own_data.T, precision=high)
    gram, raw_cross = packed_total((gram_part, raw_part), ("cells_0", "cells_1"))
    lower = jnp.linalg.cholesky(gram)
    basis = jax.scipy.linalg.solve_triangular(lower, range_rows, lower=True)
    cross = jax.scipy.linalg.solve_triangular(lower, raw_cross, lower=True)
    received = from_behind(cross, "side", 1)
    projected = jnp.dot(received, own_data, precision=high)
    result = jnp.where(side_index == 0, basis * scale, projected / scale)
    return result[None]


def solution(mesh):
    split = Mesh(
        mesh.devices.reshape(mesh.shape["groups"], 32, 4, mesh.shape["side"]),
        ("groups", "cells_0", "cells_1", "side"),
    )
    return jax.shard_map(
        per_device,
        mesh=split,
        in_specs=(P("side", None, GROUPS_CELLS), P(None, GROUPS_CELLS)),
        out_specs=P("side", None, GROUPS_CELLS),
        check_vma=False,
    )
```

profile of v0, /device:TPU:33, one launch (start us, length us, event | category | flops | bytes accessed | tf_op | source)
XLA Modules:
  0.0 273.9 jit_solution(15103181655221874833)
XLA Ops:
  0.0 0.0 copy-start
  0.0 0.9 copy-done
  0.9 5.9 %fusion.6 = f32[64,2000]{1,0:T(8,128)S(1)} fusion(f32[64,512]{1,0:T(8,128)S(1)} %copy-done, f32[1,2000,512]{2,1,0:T(8,128)} %param.2), kind=kOutput, calls=%fused_computation.6 | convolution fusion | flops 786432000 | bytes 4739072 | tf_op jit(solution)/shard_map/dot_general | solution.py:85
  6.8 0.4 reshape_reshape.9
  7.2 0.3 copy.24
  7.5 11.8 %all_to_all.50 = f32[4,32,1000]{2,1,0:T(8,128)S(1)} all-to-all(f32[4,32,1000]{2,1,0:T(8,128)S(1)} %bitcast.49), channel_id=1, replica_groups=mesh['groups'=2,'cells_0'=32,'cells_1'=4,'side'=2] {'cells_1'}, dimensions={0} | all-to-all | bytes 1024000 | tf_op jit(solution)/shard_map/all_to_all | solution.py:42
  19.4 0.1 all_to_all.33
  19.5 74.7 %all_to_all.51 = f32[32,1,1000]{2,1,0:T(1,128)S(1)} all-to-all(f32[32,1,1000]{2,1,0:T(1,128)S(1)} %all_to_all.33), channel_id=1, replica_groups=mesh['groups'=2,'cells_0'=32,'cells_1'=4,'side'=2] {'cells_0'}, dimensions={0} | all-to-all | bytes 256000 | tf_op jit(solution)/shard_map/all_to_all | solution.py:49
  94.1 0.1 reduce_sum.37
  94.2 0.1 broadcast_in_dim.15
  94.3 32.3 %all_to_all.52 = f32[32,1,1000]{2,1,0:T(1,128)S(1)} all-to-all(f32[32,1,1000]{2,1,0:T(1,128)S(1)} %broadcast_in_dim.15), channel_id=1, replica_groups=mesh['groups'=2,'cells_0'=32,'cells_1'=4,'side'=2] {'cells_0'}, dimensions={0} | all-to-all | bytes 256000 | tf_op jit(solution)/shard_map/all_to_all | solution.py:18
  126.7 9.4 %all_to_all.53 = f32[4,32,1000]{2,1,0:T(8,128)S(1)} all-to-all(f32[4,32,1000]{2,1,0:T(8,128)S(1)} %broadcast_in_dim.18), channel_id=1, replica_groups=mesh['groups'=2,'cells_0'=32,'cells_1'=4,'side'=2] {'cells_1'}, dimensions={0} | all-to-all | bytes 1024000 | tf_op jit(solution)/shard_map/all_to_all | solution.py:18
  136.0 0.3 copy.12
  136.4 0.4 reshape_reshape_reshape.3
  136.8 8.1 %collective-permute-start = (f32[64,2000]{1,0:T(8,128)S(1)}, f32[64,2000]{1,0:T(8,128)S(1)}, u32[]{:S(2)}, u32[]{:S(2)}) collective-permute-start(f32[64,2000]{1,0:T(8,128)S(1)} %reshape_reshape_reshape.3), channel_id=1, source_target_pairs={{1,0},{3,2},{5,4},{7,6},{9,8},{11,10},{13,12},{15,14},{17,16},{19,... | collective-permute-start | bytes 1536008 | tf_op jit(solution)/shard_map/ppermute | solution.py:62
  144.9 0.0 copy-start.1
  144.9 1.3 collective-permute-done
  146.2 4.7 %fusion.4 = f32[64,512]{1,0:T(8,128)S(1)} fusion(f32[1,2000,512]{2,1,0:T(8,128)} %param.2, f32[64,2000]{1,0:T(8,128)S(1)} %collective-permute-done, f32[64,2000]{1,0:T(8,128)S(1)} %reshape_reshape_reshape.3, pred[]{:T(512)S(6)} %eq.4), kind=kOutput, calls=%fused_computation.4 | convolution fusion | flops 786560000 | bytes 5251073 | tf_op jit(solution)/shard_map/dot_general | solution.py:89
  151.0 0.0 copy-done.1
  151.0 3.8 %fusion.2 = f32[64,2000]{1,0:T(8,128)S(1)} fusion(f32[64,512]{1,0:T(8,128)S(1)} %fusion.4, f32[1,2000,512]{2,1,0:T(8,128)S(1)} %copy-done.1), kind=kOutput, calls=%fused_computation.2 | convolution fusion | flops 786432000 | bytes 4739072 | tf_op jit(solution)/shard_map/dot_general | solution.py:91
  154.8 0.3 fusion.24
  155.0 0.5 reshape.48
  155.5 0.1 reshape.47
  155.6 0.5 reshape_reshape.10
  156.2 12.0 %all_to_all.54 = f32[4,32,1032]{2,1,0:T(8,128)S(1)} all-to-all(f32[4,32,1032]{2,1,0:T(8,128)S(1)} %copy.13), channel_id=1, replica_groups=mesh['groups'=2,'cells_0'=32,'cells_1'=4,'side'=2] {'cells_1'}, dimensions={0} | all-to-all | bytes 1056768 | tf_op jit(solution)/shard_map/all_to_all | solution.py:42
  168.3 0.1 all_to_all.38
  168.4 33.7 %all_to_all.55 = f32[32,1,1032]{2,1,0:T(1,128)S(1)} all-to-all(f32[32,1,1032]{2,1,0:T(1,128)S(1)} %all_to_all.38), channel_id=1, replica_groups=mesh['groups'=2,'cells_0'=32,'cells_1'=4,'side'=2] {'cells_0'}, dimensions={0} | all-to-all | bytes 264192 | tf_op jit(solution)/shard_map/all_to_all | solution.py:49
  202.1 0.1 reduce_sum.39
  202.2 0.1 broadcast_in_dim.36
  202.3 33.3 %all_to_all.56 = f32[32,1,1032]{2,1,0:T(1,128)S(1)} all-to-all(f32[32,1,1032]{2,1,0:T(1,128)S(1)} %broadcast_in_dim.36), channel_id=1, replica_groups=mesh['groups'=2,'cells_0'=32,'cells_1'=4,'side'=2] {'cells_0'}, dimensions={0} | all-to-all | bytes 264192 | tf_op jit(solution)/shard_map/all_to_all | solution.py:18
  235.7 9.7 %all_to_all.57 = f32[4,32,1032]{2,1,0:T(8,128)S(1)} all-to-all(f32[4,32,1032]{2,1,0:T(8,128)S(1)} %broadcast_in_dim.38), channel_id=1, replica_groups=mesh['groups'=2,'cells_0'=32,'cells_1'=4,'side'=2] {'cells_1'}, dimensions={0} | all-to-all | bytes 1056768 | tf_op jit(solution)/shard_map/all_to_all | solution.py:18
  245.4 0.4 copy.14
  245.8 0.8 slice.27
  246.5 0.4 reshape_reshape.11
  247.0 0.1 copy.20
  247.0 5.8 %cholesky.16 = f32[64,64]{1,0:T(8,128)S(1)} custom-call(f32[64,64]{1,0:T(8,128)S(1)} %fusion.23), custom_call_target="Cholesky" | custom-call | tf_op jit(solution)/shard_map/jit(cholesky)/cholesky | solution.py:93
  252.9 0.6 compare_reduce_fusion
  253.6 0.7 fusion.19
  254.2 4.9 %custom-call.10 = f32[1,64,64]{1,2,0:T(8,128)S(1)} custom-call(f32[1,64,64]{2,1,0:T(8,128)S(1)} %fusion.19), custom_call_target="InvertDiagBlocksLowerTriangular" | custom-call | tf_op jit(solution)/shard_map/jit(_solve_triangular)/triangular_solve | solution.py:94
  259.2 0.4 reshape.49
  259.6 0.6 fusion.20
  260.2 1.3 collective-permute-start.1
  261.5 0.3 convolution_multiply_fusion
  261.8 6.7 %collective-permute-done.1 = f32[64,2000]{1,0:T(8,128)S(1)} collective-permute-done((f32[64,2000]{1,0:T(8,128)S(1)}, f32[64,2000]{1,0:T(8,128)S(1)}, u32[]{:S(2)}, u32[]{:S(2)}) %collective-permute-start.1) | collective-permute-done | bytes 512032 | tf_op jit(solution)/shard_map/ppermute | solution.py:62
  268.5 5.4 %fusion.14 = f32[1,64,512]{2,1,0:T(8,128)} fusion(f32[64,512]{1,0:T(8,128)S(1)} %convolution_multiply_fusion, f32[64,2000]{1,0:T(8,128)S(1)} %collective-permute-done.1, f32[1,2000,512]{2,1,0:T(8,128)} %param.2, pred[]{:T(512)S(6)} %eq.4), kind=kOutput, calls=%fused_computation.10 | convolution fusion | flops 786497536 | bytes 4870145 | tf_op jit(solution)/shard_map/dot_general | solution.py:97
  (12 shorter events, 0.4 us)
Async XLA Ops:
  0.0 0.9 copy-start
  136.8 9.4 %collective-permute-start = (f32[64,2000]{1,0:T(8,128)S(1)}, f32[64,2000]{1,0:T(8,128)S(1)}, u32[]{:S(2)}, u32[]{:S(2)}) collective-permute-start(f32[64,2000]{1,0:T(8,128)S(1)} %reshape_reshape_reshape.3), channel_id=1, source_target_pairs={{1,0},{3,2},{5,4},{7,6},{9,8},{11,10},{13,12},{15,14},{17,16},{19,... | collective-permute-start | bytes 1536008 | tf_op jit(solution)/shard_map/ppermute | solution.py:62
  144.9 6.1 %copy-start.1 = (f32[1,2000,512]{2,1,0:T(8,128)S(1)}, f32[1,2000,512]{2,1,0:T(8,128)}, u32[]{:S(2)}) copy-start(f32[1,2000,512]{2,1,0:T(8,128)} %param.2) | copy-start | bytes 12288004
  260.2 8.3 %collective-permute-start.1 = (f32[64,2000]{1,0:T(8,128)S(1)}, f32[64,2000]{1,0:T(8,128)S(1)}, u32[]{:S(2)}, u32[]{:S(2)}) collective-permute-start(f32[64,2000]{1,0:T(8,128)S(1)} %fusion.20), channel_id=1, source_target_pairs={{0,1},{2,3},{4,5},{6,7},{8,9},{10,11},{12,13},{14,15},{16,17},{18,... | collective-permute-start | bytes 1536008 | tf_op jit(solution)/shard_map/ppermute | solution.py:62
where the time goes:
time: 274 us
  blocking collectives  217 us (79%)
  matrix products  21 us (8%)
  other arithmetic  12.4 us (5%)
  starting transfers between devices  9.41 us (3%)
  waiting for transfers between devices  7.96 us (3%)
  local copies, waits for them, and re-layouts  5.94 us (2%)
    all_to_all x2, blocking collectives, sum_in_two_steps(): return jnp.sum(lax.all_to_all(own, far, 0, 0, tiled=True), axis=0)  108 us
    all_to_all x4, blocking collectives, sent_to_all(): lax.all_to_all(jnp.broadcast_to(x[None], (peers, *x.shape)), axis, 0, 0,...  84.7 us
    all_to_all x2, blocking collectives, sent_and_summed(): blocks = lax.all_to_all(split_up(x, dim, peers), axis, 0, 0, tiled=True)  23.9 us
    ppermute x2, starting transfers between devices, from_behind(): lax.ppermute(value, axis, [(source, source + steps) for source in range(i...  9.41 us
    ppermute x2, waiting for transfers between devices, from_behind(): lax.ppermute(value, axis, [(source, source + steps) for source in range(i...  7.96 us
    another operation x3, other arithmetic, per_device(): lower = jnp.linalg.cholesky(gram)  6.52 us
    dot_general x1, matrix products, per_device(): partial_value = jnp.dot(sketch, own_data.T, precision=high)  5.88 us
    another operation x2, other arithmetic, per_device(): basis = jax.scipy.linalg.solve_triangular(lower, range_rows, lower=True)  5.55 us
  transfers between devices with their start and end apart: 2, of which 2 were waited for; matrix products, arithmetic and copies ran while one was open for 0% of the time, Pallas kernels for 0%

commit v1 on v0

v1 whole, which is shorter than its diff:
```python
import jax
import jax.numpy as jnp
from jax import lax
from jax.sharding import Mesh
from jax.sharding import PartitionSpec as P

Z_LOW = 4
X_SIZE = 4
GROUPS_CELLS = ("groups", "z_high", "z_low", "x")
NEAR = ("z_low", "x")
FAR = "z_high"
ROWS = 8


def exchanged(blocks, axes):
    return lax.all_to_all(blocks, axes, 0, 0, tiled=True)


def to_all(x, axes):
    return exchanged(jnp.broadcast_to(x[None], (lax.axis_size(axes), *x.shape)), axes)


def sum_over_cells(half):
    rows, cols = half.shape
    part = cols // Z_LOW
    blocks = half.reshape(X_SIZE, ROWS, Z_LOW, part).transpose(2, 0, 1, 3)
    blocks = blocks.reshape(Z_LOW * X_SIZE, ROWS, part)
    own = jnp.sum(exchanged(blocks, NEAR), axis=0)
    own = jnp.sum(to_all(own, FAR), axis=0)
    whole = to_all(own, NEAR).reshape(Z_LOW, X_SIZE, ROWS, part)
    return whole.transpose(1, 2, 0, 3).reshape(rows, cols)


def per_device(datasets, sketch):
    high = lax.Precision.HIGHEST
    own_data = datasets[0]
    genes = own_data.shape[0]
    k = sketch.shape[0]
    half = k // 2
    wide = -(-(genes + 48) // (128 * Z_LOW)) * 128 * Z_LOW
    on_x = lax.axis_index("side") == 0
    cell_count = own_data.shape[1] * lax.axis_size(GROUPS_CELLS[1:])
    scale = jnp.sqrt(jnp.float32(cell_count))

    partial_panel = jnp.dot(sketch, own_data.T, precision=high)
    partial_panel = jnp.pad(partial_panel, ((0, 0), (0, wide - genes)))
    moved = lax.ppermute(partial_panel[:half], "side", [(1, 0)])
    mine = sum_over_cells(jnp.where(on_x, moved, partial_panel[half:]))
    other = lax.ppermute(mine, "side", [(1, 0)])
    panel = jnp.concatenate([mine, other])[:, :genes]

    range_rows = jnp.dot(panel, own_data, precision=high)
    gram = jnp.dot(range_rows, range_rows.T, precision=high)
    corner = gram[half:, half:]
    packed = jnp.concatenate([gram[:, :half], jnp.concatenate([corner[:, : half // 2], corner[:, half // 2 :]])], axis=1)
    raw = jnp.dot(range_rows, own_data.T, precision=high)
    raw = jnp.concatenate([raw, packed, jnp.zeros((k, wide - genes - packed.shape[1]), raw.dtype)], axis=1)
    moved = lax.ppermute(raw[half:], "side", [(0, 1)])
    mine = sum_over_cells(jnp.where(on_x, raw[:half], moved))
    other = lax.ppermute(mine, "side", [(0, 1), (1, 0)])
    total = jnp.concatenate([jnp.where(on_x, mine, other), jnp.where(on_x, other, mine)])

    raw_cross = total[:, :genes]
    packed = total[:, genes : genes + half + half // 2]
    corner = packed[:, half:]
    corner = jnp.concatenate([corner[:half], corner[half:]], axis=1)
    gram = jnp.concatenate([packed[:, :half], jnp.concatenate([jnp.zeros_like(corner), corner])], axis=1)
    lower = lax.linalg.cholesky(gram, symmetrize_input=False)
    inverse = jax.scipy.linalg.solve_triangular(lower, jnp.eye(k, dtype=gram.dtype), lower=True)
    cross = jnp.dot(inverse, raw_cross, precision=high)
    left = jnp.where(on_x, inverse * scale, 0)
    basis = jnp.dot(left, range_rows, precision=high)
    projected = jnp.dot(cross, own_data, precision=high)
    return jnp.where(on_x, basis, projected / scale)[None]


def solution(mesh):
    devices = mesh.devices.reshape(mesh.shape["groups"], -1, Z_LOW, X_SIZE, mesh.shape["side"])
    split = Mesh(devices, (*GROUPS_CELLS, "side"))
    return jax.shard_map(
        per_device,
        mesh=split,
        in_specs=(P("side", None, GROUPS_CELLS), P(None, GROUPS_CELLS)),
        out_specs=P("side", None, GROUPS_CELLS),
        check_vma=False,
    )
```

time: 274 us -> 217 us (0.79)
  blocking collectives: 217 us -> 118 us
  starting transfers between devices: 9.41 us -> 57.4 us
  local copies, waits for them, and re-layouts: 5.94 us -> 1.81 us
    all_to_all x8 -> x6, blocking collectives: 217 us -> 118 us  [exchanged(): return lax.all_to_all(blocks, axes, 0, 0, tiled=True)]
    ppermute x2 -> x4, starting transfers between devices: 9.41 us -> 57.4 us  [the longest x1 43.4 us: per_device(): moved = lax.ppermute(partial_panel[:half], 'side', [(1, 0)])]
    ppermute x2 -> x4, waiting for transfers between devices: 7.96 us -> 5.54 us  [the longest x1 2.14 us: per_device(): moved = lax.ppermute(raw[half:], 'side', [(0, 1)])]
    dot_general x4 -> x6, matrix products: 15.3 us -> 16.2 us  [the longest x1 5.88 us: per_device(): partial_panel = jnp.dot(sketch, own_data.T, precision=high)]
  transfers between devices with their start and end apart: 2 -> 4, of which waited for: 2 -> 4; matrix products, arithmetic and copies ran while one was open for 0% -> 0% of each run, Pallas kernels for 0% -> 0%
where the time goes in v1:
time: 217 us; the launch traced here: 216 us
  blocking collectives  118 us (54%)
  starting transfers between devices  57.4 us (26%)
  matrix products  21.2 us (10%)
  other arithmetic  12.5 us (6%)
  waiting for transfers between devices  5.54 us (3%)
    all_to_all x6, blocking collectives, exchanged(): return lax.all_to_all(blocks, axes, 0, 0, tiled=True)  118 us
    ppermute x1, starting transfers between devices, per_device(): moved = lax.ppermute(partial_panel[:half], 'side', [(1, 0)])  43.4 us
    ppermute x1, starting transfers between devices, per_device(): other = lax.ppermute(mine, 'side', [(1, 0)])  7.09 us
    another operation x3, other arithmetic, per_device(): lower = lax.linalg.cholesky(gram, symmetrize_input=False)  6.52 us
    dot_general x1, matrix products, per_device(): partial_panel = jnp.dot(sketch, own_data.T, precision=high)  5.88 us
    ppermute x1, starting transfers between devices, per_device(): other = lax.ppermute(mine, 'side', [(0, 1), (1, 0)])  5.59 us
    another operation x2, other arithmetic, per_device(): jax.scipy.linalg.solve_triangular(lower, jnp.eye(k, dtype=gram.dtype), lo...  5.55 us
    dot_general x1, matrix products, per_device(): projected = jnp.dot(cross, own_data, precision=high)  5.43 us
  transfers between devices with their start and end apart: 4, of which 4 were waited for; matrix products, arithmetic and copies ran while one was open for 0% of the time, Pallas kernels for 0%

profile of v1, /device:TPU:33, one launch (start us, length us, event | category | flops | bytes accessed | tf_op | source)
XLA Modules:
  0.0 216.5 jit_solution(9260297536390134471)
XLA Ops:
  0.0 0.0 copy-start
  0.0 0.9 copy-done
  0.9 5.9 %fusion.6 = f32[64,2000]{1,0:T(8,128)S(1)} fusion(f32[64,512]{1,0:T(8,128)S(1)} %copy-done, f32[1,2000,512]{2,1,0:T(8,128)} %param.2), kind=kOutput, calls=%fused_computation.6 | convolution fusion | flops 786432000 | bytes 4739072 | tf_op jit(solution)/shard_map/dot_general | solution.py:45
  6.8 43.4 %collective-permute-start = (f32[32,2048]{1,0:T(8,128)S(1)}, f32[32,2048]{1,0:T(8,128)S(1)}, u32[]{:S(2)}, u32[]{:S(2)}) collective-permute-start(f32[32,2048]{1,0:T(8,128)S(1)} %pad_slice_fusion.1), channel_id=1, source_target_pairs={{1,0},{3,2},{5,4},{7,6},{9,8},{11,10},{13,12},{15,14},{17,16},{19,... | collective-permute-start | bytes 786440 | tf_op jit(solution)/shard_map/ppermute | solution.py:47
  50.2 1.1 collective-permute-done
  51.4 12.9 %all_to_all.30 = f32[16,8,512]{2,1,0:T(8,128)S(1)} all-to-all(f32[16,8,512]{2,1,0:T(8,128)S(1)} %bitcast.51), channel_id=1, replica_groups=mesh['groups'=2,'z_high'=8,'z_low'=4,'x'=4,'side'=2] {'z_low','x'}, dimensions={0} | all-to-all | bytes 524288 | tf_op jit(solution)/shard_map/all_to_all | solution.py:16
  64.3 32.1 %all_to_all.31 = f32[8,8,512]{2,1,0:T(8,128)S(1)} all-to-all(f32[8,8,512]{2,1,0:T(8,128)S(1)} %broadcast_in_dim.11), channel_id=1, replica_groups=mesh['groups'=2,'z_high'=8,'z_low'=4,'x'=4,'side'=2] {'z_high'}, dimensions={0} | all-to-all | bytes 262144 | tf_op jit(solution)/shard_map/all_to_all | solution.py:16
  96.4 0.0 copy-start.1
  96.5 15.8 %all_to_all.32 = f32[16,8,512]{2,1,0:T(8,128)S(1)} all-to-all(f32[16,8,512]{2,1,0:T(8,128)S(1)} %broadcast_in_dim.12), channel_id=1, replica_groups=mesh['groups'=2,'z_high'=8,'z_low'=4,'x'=4,'side'=2] {'z_low','x'}, dimensions={0} | all-to-all | bytes 524288 | tf_op jit(solution)/shard_map/all_to_all | solution.py:16
  112.3 0.2 copy.34
  112.5 0.1 copy.32
  112.6 7.1 %collective-permute-start.1 = (f32[32,2048]{1,0:T(8,128)S(1)}, f32[32,2048]{1,0:T(8,128)S(1)}, u32[]{:S(2)}, u32[]{:S(2)}) collective-permute-start(f32[32,2048]{1,0:T(8,128)S(1)} %bitcast.49), channel_id=1, source_target_pairs={{1,0},{3,2},{5,4},{7,6},{9,8},{11,10},{13,12},{15,14},{17,16},{19,... | collective-permute-start | bytes 786440 | tf_op jit(solution)/shard_map/ppermute | solution.py:49
  119.7 1.1 collective-permute-done.1
  120.8 4.8 %fusion.4 = f32[64,512]{1,0:T(8,128)S(1)} fusion(f32[1,2000,512]{2,1,0:T(8,128)} %param.2, f32[32,2048]{1,0:T(8,128)S(1)} %collective-permute-done.1, f32[32,2048]{1,0:T(8,128)S(1)} %bitcast.50), kind=kOutput, calls=%fused_computation.4 | convolution fusion | flops 786560000 | bytes 4751360 | tf_op jit(solution)/shard_map/dot_general | solution.py:52
  125.6 0.3 fusion.36
  125.8 0.1 fusion.35
  125.9 0.0 copy-done.1
  125.9 3.8 %fusion.2 = f32[64,2000]{1,0:T(8,128)S(1)} fusion(f32[64,512]{1,0:T(8,128)S(1)} %fusion.4, f32[1,2000,512]{2,1,0:T(8,128)S(1)} %copy-done.1), kind=kOutput, calls=%fused_computation.2 | convolution fusion | flops 786432000 | bytes 4739072 | tf_op jit(solution)/shard_map/dot_general | solution.py:56
  129.7 0.1 copy.31
  129.8 0.1 pad_maximum_fusion.4
  129.8 0.1 copy.28
  129.9 0.1 concatenate.23
  130.1 1.3 collective-permute-start.2
  131.4 2.1 collective-permute-done.2
  133.6 13.0 %all_to_all.33 = f32[16,8,512]{2,1,0:T(8,128)S(1)} all-to-all(f32[16,8,512]{2,1,0:T(8,128)S(1)} %bitcast.53), channel_id=1, replica_groups=mesh['groups'=2,'z_high'=8,'z_low'=4,'x'=4,'side'=2] {'z_low','x'}, dimensions={0} | all-to-all | bytes 524288 | tf_op jit(solution)/shard_map/all_to_all | solution.py:16
  146.6 27.6 %all_to_all.34 = f32[8,8,512]{2,1,0:T(8,128)S(1)} all-to-all(f32[8,8,512]{2,1,0:T(8,128)S(1)} %broadcast_in_dim.13), channel_id=1, replica_groups=mesh['groups'=2,'z_high'=8,'z_low'=4,'x'=4,'side'=2] {'z_high'}, dimensions={0} | all-to-all | bytes 262144 | tf_op jit(solution)/shard_map/all_to_all | solution.py:16
  174.3 16.5 %all_to_all.35 = f32[16,8,512]{2,1,0:T(8,128)S(1)} all-to-all(f32[16,8,512]{2,1,0:T(8,128)S(1)} %broadcast_in_dim.14), channel_id=1, replica_groups=mesh['groups'=2,'z_high'=8,'z_low'=4,'x'=4,'side'=2] {'z_low','x'}, dimensions={0} | all-to-all | bytes 524288 | tf_op jit(solution)/shard_map/all_to_all | solution.py:16
  190.8 5.6 %collective-permute-start.3 = (f32[32,2048]{1,0:T(8,128)S(1)}, f32[32,2048]{1,0:T(8,128)S(1)}, u32[]{:S(2)}, u32[]{:S(2)}) collective-permute-start(f32[32,2048]{1,0:T(8,128)S(1)} %bitcast.55), channel_id=1, source_target_pairs={{0,1},{1,0},{2,3},{3,2},{4,5},{5,4},{6,7},{7,6},{8,9},{9,8},{10,11... | collective-permute-start | bytes 786440 | tf_op jit(solution)/shard_map/ppermute | solution.py:60
  196.4 1.1 collective-permute-done.3
  197.6 0.1 slice.74
  197.6 0.1 slice.75
  197.7 0.1 select_maximum_fusion
  197.8 0.1 fusion.22
  197.9 5.8 %cholesky.17 = f32[64,64]{1,0:T(8,128)S(1)} custom-call(f32[64,64]{1,0:T(8,128)S(1)} %fusion.22), custom_call_target="Cholesky" | custom-call | tf_op jit(solution)/shard_map/cholesky | solution.py:68
  203.8 0.6 compare_reduce_fusion
  204.4 0.7 fusion.21
  205.1 4.9 %custom-call.6 = f32[1,64,64]{1,2,0:T(8,128)S(1)} custom-call(f32[1,64,64]{2,1,0:T(8,128)S(1)} %fusion.21), custom_call_target="InvertDiagBlocksLowerTriangular" | custom-call | tf_op jit(solution)/shard_map/jit(_solve_triangular)/triangular_solve | solution.py:69
  210.0 0.2 fusion.23
  210.2 0.6 fusion.17
  210.8 0.3 fusion.25
  211.1 5.4 %fusion.14 = f32[1,64,512]{2,1,0:T(8,128)} fusion(f32[64,512]{1,0:T(8,128)S(1)} %fusion.25, f32[64,2000]{1,0:T(8,128)S(1)} %fusion.17, f32[1,2000,512]{2,1,0:T(8,128)} %param.2, pred[]{:T(512)S(6)} %eq.4), kind=kOutput, calls=%fused_computation.10 | convolution fusion | flops 786497536 | bytes 4870145 | tf_op jit(solution)/shard_map/dot_general | solution.py:73
  (18 shorter events, 0.4 us)
Async XLA Ops:
  0.0 0.9 copy-start
  6.8 44.5 %collective-permute-start = (f32[32,2048]{1,0:T(8,128)S(1)}, f32[32,2048]{1,0:T(8,128)S(1)}, u32[]{:S(2)}, u32[]{:S(2)}) collective-permute-start(f32[32,2048]{1,0:T(8,128)S(1)} %pad_slice_fusion.1), channel_id=1, source_target_pairs={{1,0},{3,2},{5,4},{7,6},{9,8},{11,10},{13,12},{15,14},{17,16},{19,... | collective-permute-start | bytes 786440 | tf_op jit(solution)/shard_map/ppermute | solution.py:47
  96.4 29.5 %copy-start.1 = (f32[1,2000,512]{2,1,0:T(8,128)S(1)}, f32[1,2000,512]{2,1,0:T(8,128)}, u32[]{:S(2)}) copy-start(f32[1,2000,512]{2,1,0:T(8,128)} %param.2) | copy-start | bytes 12288004
  112.6 8.2 %collective-permute-start.1 = (f32[32,2048]{1,0:T(8,128)S(1)}, f32[32,2048]{1,0:T(8,128)S(1)}, u32[]{:S(2)}, u32[]{:S(2)}) collective-permute-start(f32[32,2048]{1,0:T(8,128)S(1)} %bitcast.49), channel_id=1, source_target_pairs={{1,0},{3,2},{5,4},{7,6},{9,8},{11,10},{13,12},{15,14},{17,16},{19,... | collective-permute-start | bytes 786440 | tf_op jit(solution)/shard_map/ppermute | solution.py:49
  130.1 3.5 %collective-permute-start.2 = (f32[32,2048]{1,0:T(8,128)S(1)}, f32[32,2048]{1,0:T(8,128)S(1)}, u32[]{:S(2)}, u32[]{:S(2)}) collective-permute-start(f32[32,2048]{1,0:T(8,128)S(1)} %slice.73), channel_id=1, source_target_pairs={{0,1},{2,3},{4,5},{6,7},{8,9},{10,11},{12,13},{14,15},{16,17},{18,... | collective-permute-start | bytes 786440 | tf_op jit(solution)/shard_map/ppermute | solution.py:58
  190.8 6.7 %collective-permute-start.3 = (f32[32,2048]{1,0:T(8,128)S(1)}, f32[32,2048]{1,0:T(8,128)S(1)}, u32[]{:S(2)}, u32[]{:S(2)}) collective-permute-start(f32[32,2048]{1,0:T(8,128)S(1)} %bitcast.55), channel_id=1, source_target_pairs={{0,1},{1,0},{2,3},{3,2},{4,5},{5,4},{6,7},{7,6},{8,9},{9,8},{10,11... | collective-permute-start | bytes 786440 | tf_op jit(solution)/shard_map/ppermute | solution.py:60

commit v2 on v1

v2 whole, which is shorter than its diff:
```python
import functools

import jax
import jax.numpy as jnp
from jax import lax
from jax.experimental import pallas as pl
from jax.experimental.pallas import tpu as pltpu
from jax.sharding import Mesh
from jax.sharding import PartitionSpec as P

Z_LOW = 4
X_SIZE = 4
GROUPS_CELLS = ("groups", "z_high", "z_low", "x")
NEAR = ("z_low", "x")
FAR = "z_high"
ROWS = 8
LANES = 128
STEP = 256
F32 = jnp.float32
BF16 = jnp.bfloat16
HIGH = lax.Precision.HIGHEST
VMEM = pl.BlockSpec(memory_space=pltpu.VMEM)
ANY = pl.BlockSpec(memory_space=pl.ANY)
SMEM = pl.BlockSpec(memory_space=pltpu.SMEM)


def exchanged(blocks, axes):
    return lax.all_to_all(blocks, axes, 0, 0, tiled=True)


def to_all(x, axes):
    return exchanged(jnp.broadcast_to(x[None], (lax.axis_size(axes), *x.shape)), axes)


def sum_over_cells(blocks):
    own = jnp.sum(exchanged(blocks, NEAR), axis=0)
    own = jnp.sum(to_all(own, FAR), axis=0)
    return to_all(own, NEAR)


def halves(x):
    top = x.astype(BF16)
    return top, (x - top.astype(F32)).astype(BF16)


def times(a, b):
    return lax.dot_general(a, b, (((1,), (0,)), ((), ())), preferred_element_type=F32)


def times_t(a, b):
    return lax.dot_general(a, b, (((1,), (1,)), ((), ())), preferred_element_type=F32)


def three(product, stacked, top, low, k):
    both = product(stacked, top)
    return both[:k] + both[k:] + product(stacked[:k], low)


def put_blocks(send_ref, keep_ref, value, first, flip):
    width = value.shape[1]
    part = send_ref.shape[2]
    col = first % part
    half = value.shape[0] // 2
    for x in range(X_SIZE):
        b = first // part * X_SIZE + x
        upper = value[ROWS * x : ROWS * (x + 1)]
        lower = value[half + ROWS * x : half + ROWS * (x + 1)]
        send_ref[b, :, col : col + width] = lower if flip else upper
        keep_ref[b, :, col : col + width] = upper if flip else lower


def whole_rows(block_ref, z):
    return jnp.concatenate([block_ref[z * X_SIZE + x] for x in range(X_SIZE)], axis=0)


def panel_kernel(sketch_ref, data_ref, top_ref, low_ref, send_ref, keep_ref, held, sems):
    genes, cells = held.shape
    wide = top_ref.shape[0]
    k = sketch_ref.shape[0]
    copies = []
    for i, first in enumerate(range(0, genes, STEP)):
        rows = min(STEP, genes - first)
        copy = pltpu.make_async_copy(data_ref.at[0, pl.ds(first, rows)], held.at[pl.ds(first, rows)], sems.at[i])
        copy.start()
        copies.append(copy)
    top_ref[genes:] = jnp.zeros((wide - genes, cells), BF16)
    low_ref[genes:] = jnp.zeros((wide - genes, cells), BF16)
    stacked = jnp.concatenate(halves(sketch_ref[...]), axis=0)
    for i, first in enumerate(range(0, genes, STEP)):
        rows = min(STEP, genes - first)
        copies[i].wait()
        top, low = halves(held[first : first + rows])
        top_ref[first : first + rows] = top
        low_ref[first : first + rows] = low
        value = three(times_t, stacked, top_ref[first : first + STEP], low_ref[first : first + STEP], k)
        put_blocks(send_ref, keep_ref, value, first, False)


def lanes(shape):
    return lax.broadcasted_iota(jnp.int32, shape, 1)


def sublanes(shape):
    return lax.broadcasted_iota(jnp.int32, shape, 0)


def range_kernel(mine_ref, other_ref, top_ref, low_ref, rows_ref, send_ref, keep_ref, panel):
    k = rows_ref.shape[0]
    half = k // 2
    part = send_ref.shape[2]
    wide = top_ref.shape[0]
    for z in range(Z_LOW):
        cols = slice(z * part, (z + 1) * part)
        for i, ref in enumerate((mine_ref, other_ref)):
            top, low = halves(whole_rows(ref, z))
            panel[i * half : (i + 1) * half, cols] = top
            panel[k + i * half : k + (i + 1) * half, cols] = low
    rows = three(times, panel[...], top_ref[...], low_ref[...], k)
    rows_ref[...] = rows
    stacked = jnp.concatenate(halves(rows), axis=0)
    padded = jnp.concatenate([rows, jnp.zeros((LANES - k, rows.shape[1]), F32)], axis=0)
    gram = lax.dot_general(rows, padded, (((1,), (1,)), ((), ())), precision=HIGH, preferred_element_type=F32)
    near = pltpu.roll(gram, LANES - half - half // 2, 1)
    far = pltpu.roll(gram, LANES - k, 1)
    lane, row = lanes(near.shape), sublanes(near.shape)
    far = jnp.concatenate([far[half:], far[half:]], axis=0)
    packed = jnp.where((lane >= LANES - half // 2) & (row < half), far, near)
    for z in range(Z_LOW):
        cols = slice(z * part, (z + 1) * part)
        value = three(times_t, stacked, top_ref[cols], low_ref[cols], k)
        if z < Z_LOW - 1:
            put_blocks(send_ref, keep_ref, value, z * part, True)
        else:
            last = value[:, part - LANES :]
            last = jnp.where(lane >= LANES - half - half // 2, packed, last)
            put_blocks(send_ref, keep_ref, value[:, : part - LANES], z * part, True)
            put_blocks(send_ref, keep_ref, last, wide - LANES, True)


def factor_inverse(packed, k):
    half = k // 2
    lane, row = lanes((k, LANES)), sublanes((k, LANES))
    near = pltpu.roll(packed, half + half // 2, 1)
    far = pltpu.roll(packed, k, 1)
    far = jnp.concatenate([far[:half], far[:half]], axis=0)
    square = jnp.where(lane >= half + half // 2, far, near)
    square = jnp.where((lane < half) | ((lane < k) & (row >= half)), square, 0.0)
    full = jnp.concatenate([square, jnp.zeros((LANES - k, LANES), F32)], axis=0)
    square = jnp.where((lane >= half) & (lane < k) & (row < half), full.T[:k], square)
    work = jnp.where(lane == row + k, 1.0, square)
    pivots = jnp.ones((k, LANES), F32)
    for j in range(k):
        base = j // ROWS * ROWS
        pivot_row = jnp.broadcast_to(work[j : j + 1], (ROWS, LANES))
        pivot = jnp.broadcast_to(pivot_row[:, j : j + 1], (ROWS, LANES))
        scaled = pivot_row / pivot
        pivots = jnp.where(row == j, jnp.concatenate([pivot] * (k // ROWS), axis=0), pivots)
        below = work[base:]
        column = jnp.where(row[base:] > j, jnp.broadcast_to(below[:, j : j + 1], below.shape), 0.0)
        below = below - column * jnp.concatenate([scaled] * ((k - base) // ROWS), axis=0)
        work = below if base == 0 else jnp.concatenate([work[:base], below], axis=0)
    inverse = pltpu.roll(work * lax.rsqrt(pivots), LANES - k, 1)
    return jnp.where(lane < k, inverse, 0.0)


def factor_kernel(scale, side_ref, mine_ref, other_ref, rows_ref, top_ref, low_ref, out_ref, total, stacked):
    k = rows_ref.shape[0]
    half = k // 2
    wide = top_ref.shape[0]
    part = mine_ref.shape[2]
    on_x = side_ref[0] == 0
    for z in range(Z_LOW):
        cols = slice(z * part, (z + 1) * part)
        mine, other = whole_rows(mine_ref, z), whole_rows(other_ref, z)
        total[:half, cols] = jnp.where(on_x, mine, other)
        total[half:, cols] = jnp.where(on_x, other, mine)
    inverse = factor_inverse(total[:, wide - LANES :], k)[:, :k]

    @pl.when(on_x)
    def _():
        out_ref[0] = lax.dot_general(inverse * scale, rows_ref[...], (((1,), (0,)), ((), ())), precision=HIGH, preferred_element_type=F32)

    @pl.when(jnp.logical_not(on_x))
    def _():
        for z in range(Z_LOW):
            cols = slice(z * part, (z + 1) * part)
            cross = lax.dot_general(inverse, total[:, cols], (((1,), (0,)), ((), ())), precision=HIGH, preferred_element_type=F32)
            top, low = halves(cross)
            stacked[:k, cols] = top
            stacked[k:, cols] = low
        out_ref[0] = three(times, stacked[...], top_ref[...], low_ref[...], k) * (1.0 / scale)


def per_device(datasets, sketch):
    _, genes, cells = datasets.shape
    k = sketch.shape[0]
    wide = -(-(genes + k * 3 // 4) // (LANES * Z_LOW)) * LANES * Z_LOW
    near_count = Z_LOW * X_SIZE
    blocks = jax.ShapeDtypeStruct((near_count, ROWS, wide // Z_LOW), F32)
    parts = jax.ShapeDtypeStruct((wide, cells), BF16)
    on_x = lax.axis_index("side") == 0
    scale = float(cells * lax.axis_size(GROUPS_CELLS[1:])) ** 0.5
    count = -(-genes // STEP)

    top, low, send, keep = pl.pallas_call(
        panel_kernel,
        in_specs=[VMEM, ANY],
        out_specs=[VMEM] * 4,
        out_shape=[parts, parts, blocks, blocks],
        scratch_shapes=[pltpu.VMEM((genes, cells), F32), pltpu.SemaphoreType.DMA((count,))],
        name="panel",
    )(sketch, datasets)
    moved = lax.ppermute(send, "side", [(1, 0)])
    mine = sum_over_cells(jnp.where(on_x, moved, keep))
    other = lax.ppermute(mine, "side", [(1, 0)])

    rows, send, keep = pl.pallas_call(
        range_kernel,
        in_specs=[VMEM] * 4,
        out_specs=[VMEM] * 3,
        out_shape=[jax.ShapeDtypeStruct((k, cells), F32), blocks, blocks],
        scratch_shapes=[pltpu.VMEM((2 * k, wide), BF16)],
        name="range_rows",
    )(mine, other, top, low)
    moved = lax.ppermute(send, "side", [(0, 1)])
    mine = sum_over_cells(jnp.where(on_x, keep, moved))
    other = lax.ppermute(mine, "side", [(0, 1), (1, 0)])

    side = lax.axis_index("side").astype(jnp.int32).reshape(1)
    return pl.pallas_call(
        functools.partial(factor_kernel, scale),
        in_specs=[SMEM] + [VMEM] * 5,
        out_specs=VMEM,
        out_shape=jax.ShapeDtypeStruct((1, k, cells), F32),
        scratch_shapes=[pltpu.VMEM((k, wide), F32), pltpu.VMEM((2 * k, wide), BF16)],
        name="factor",
    )(side, mine, other, rows, top, low)


def solution(mesh):
    devices = mesh.devices.reshape(mesh.shape["groups"], -1, Z_LOW, X_SIZE, mesh.shape["side"])
    split = Mesh(devices, (*GROUPS_CELLS, "side"))
    return jax.shard_map(
        per_device,
        mesh=split,
        in_specs=(P("side", None, GROUPS_CELLS), P(None, GROUPS_CELLS)),
        out_specs=P("side", None, GROUPS_CELLS),
        check_vma=False,
    )
```

time: 217 us -> 209 us (0.963)
  Pallas kernels: 0 us -> 25.3 us
  matrix products: 21.2 us -> 0 us
  other arithmetic: 12.5 us -> 1.1 us
    pallas_call x0 -> x3, Pallas kernels: none -> 25.3 us  [the longest x1 12.9 us: per_device(): pl.pallas_call(functools.partial(factor_kernel, scale), in_specs=[SMEM] +...]
    dot_general x7 -> x0, matrix products: 20.9 us -> none  [the longest x1 5.88 us: per_device(): partial_panel = jnp.dot(sketch, own_data.T, precision=high)]
    another operation x5 -> x0, other arithmetic: 12.1 us -> none  [the longest x3 6.52 us: per_device(): lower = lax.linalg.cholesky(gram, symmetrize_input=False)]
    ppermute x1, starting transfers between devices: 5.59 us -> 8.29 us  [per_device(): other = lax.ppermute(mine, 'side', [(0, 1), (1, 0)])]
where the time goes in v2:
time: 209 us
  blocking collectives  117 us (56%)
  starting transfers between devices  58.2 us (28%)
  Pallas kernels  25.3 us (12%)
  waiting for transfers between devices  5.95 us (3%)
    all_to_all x6, blocking collectives, exchanged(): return lax.all_to_all(blocks, axes, 0, 0, tiled=True)  117 us
    ppermute x1, starting transfers between devices, per_device(): moved = lax.ppermute(send, 'side', [(1, 0)])  43.4 us
    pallas_call x1, Pallas kernels, per_device(): pl.pallas_call(functools.partial(factor_kernel, scale), in_specs=[SMEM] +...  12.9 us
    ppermute x1, starting transfers between devices, per_device(): other = lax.ppermute(mine, 'side', [(0, 1), (1, 0)])  8.29 us
    pallas_call x1, Pallas kernels, per_device(): pl.pallas_call(panel_kernel, in_specs=[VMEM, ANY], out_specs=[VMEM] * 4,...  7.08 us
    pallas_call x1, Pallas kernels, per_device(): pl.pallas_call(range_kernel, in_specs=[VMEM] * 4, out_specs=[VMEM] * 3, o...  5.34 us
    ppermute x1, starting transfers between devices, per_device(): other = lax.ppermute(mine, 'side', [(1, 0)])  5.2 us
  transfers between devices with their start and end apart: 4, of which 4 were waited for; matrix products, arithmetic and copies ran while one was open for 0% of the time, Pallas kernels for 0%

profile of v2, /device:TPU:33, one launch (start us, length us, event | category | flops | bytes accessed | tf_op | source)
XLA Modules:
  0.0 209.0 jit_solution(5821054804698570619)
XLA Ops:
  0.0 7.1 %panel.1 = (bf16[2048,512]{1,0:T(8,128)(2,1)}, bf16[2048,512]{1,0:T(8,128)(2,1)}, f32[16,8,512]{2,1,0:T(8,128)}, f32[16,8,512]{2,1,0:T(8,128)}) custom-call(f32[64,512]{1,0:T(8,128)} %sketch_ref.1, f32[1,2000,512]{2,1,0:T(8,128)} %data_ref.1), custom_call_target="tpu_custom_call" | custom-call | tf_op jit(solution)/shard_map/panel/pallas_call | solution.py:205
  7.1 43.4 %collective-permute-start = (f32[16,8,512]{2,1,0:T(8,128)}, f32[16,8,512]{2,1,0:T(8,128)S(1)}, u32[]{:S(2)}, u32[]{:S(2)}) collective-permute-start(f32[16,8,512]{2,1,0:T(8,128)} %get-tuple-element.12), channel_id=1, source_target_pairs={{1,0},{3,2},{5,4},{7,6},{9,8},{11,10},{13,12},{15,14},{17,16},{19,... | collective-permute-start | bytes 786440 | tf_op jit(solution)/shard_map/ppermute | solution.py:213
  50.5 1.3 collective-permute-done
  51.8 1.0 broadcast_select_fusion.1
  52.8 13.8 %all_to_all.30 = f32[16,8,512]{2,1,0:T(8,128)S(1)} all-to-all(f32[16,8,512]{2,1,0:T(8,128)S(1)} %broadcast_select_fusion.1), channel_id=1, replica_groups=mesh['groups'=2,'z_high'=8,'z_low'=4,'x'=4,'side'=2] {'z_low','x'}, dimensions={0} | all-to-all | bytes 524288 | tf_op jit(solution)/shard_map/all_to_all | solution.py:28
  66.7 32.6 %all_to_all.31 = f32[8,8,512]{2,1,0:T(8,128)S(1)} all-to-all(f32[8,8,512]{2,1,0:T(8,128)S(1)} %broadcast_in_dim.8), channel_id=1, replica_groups=mesh['groups'=2,'z_high'=8,'z_low'=4,'x'=4,'side'=2] {'z_high'}, dimensions={0} | all-to-all | bytes 262144 | tf_op jit(solution)/shard_map/all_to_all | solution.py:28
  99.3 16.3 %all_to_all.32.mine_ref = f32[16,8,512]{2,1,0:T(8,128)S(1)} all-to-all(f32[16,8,512]{2,1,0:T(8,128)S(1)} %broadcast_in_dim.9), channel_id=1, replica_groups=mesh['groups'=2,'z_high'=8,'z_low'=4,'x'=4,'side'=2] {'z_low','x'}, dimensions={0} | all-to-all | bytes 524288 | tf_op jit(solution)/shard_map/all_to_all | solution.py:28
  115.6 0.0 copy-start.1
  115.7 5.2 %collective-permute-start.1 = (f32[16,8,512]{2,1,0:T(8,128)S(1)}, f32[16,8,512]{2,1,0:T(8,128)S(1)}, u32[]{:S(2)}, u32[]{:S(2)}) collective-permute-start(f32[16,8,512]{2,1,0:T(8,128)S(1)} %all_to_all.32.mine_ref), channel_id=1, source_target_pairs={{1,0},{3,2},{5,4},{7,6},{9,8},{11,10},{13,12},{15,14},{17,16},{19,... | collective-permute-start | bytes 786440 | tf_op jit(solution)/shard_map/ppermute | solution.py:215
  120.9 1.1 collective-permute-done.1.other_ref
  122.0 0.0 copy-start.3
  122.0 0.0 copy-done.1
  122.0 0.7 copy-done.3
  122.7 5.3 %range_rows.1 = (f32[64,512]{1,0:T(8,128)}, f32[16,8,512]{2,1,0:T(8,128)}, f32[16,8,512]{2,1,0:T(8,128)}) custom-call(f32[16,8,512]{2,1,0:T(8,128)} %copy-done.1, f32[16,8,512]{2,1,0:T(8,128)} %copy-done.3, bf16[2048,512]{1,0:T(8,128)(2,1)} %get-tuple-element.14.top_ref, bf16[2048,512]{1,0:T(8,128)(2,1)} %get-tuple-element.15.low_ref), custom_call_target="tpu_custom_call" | custom-call | tf_op jit(solution)/shard_map/range_rows/pallas_call | solution.py:217
  128.0 1.3 collective-permute-start.2
  129.3 2.4 %collective-permute-done.2 = f32[16,8,512]{2,1,0:T(8,128)S(1)} collective-permute-done((f32[16,8,512]{2,1,0:T(8,128)}, f32[16,8,512]{2,1,0:T(8,128)S(1)}, u32[]{:S(2)}, u32[]{:S(2)}) %collective-permute-start.2) | collective-permute-done | bytes 262176 | tf_op jit(solution)/shard_map/ppermute | solution.py:225
  131.7 11.9 %all_to_all.33 = f32[16,8,512]{2,1,0:T(8,128)S(1)} all-to-all(f32[16,8,512]{2,1,0:T(8,128)S(1)} %broadcast_select_fusion), channel_id=1, replica_groups=mesh['groups'=2,'z_high'=8,'z_low'=4,'x'=4,'side'=2] {'z_low','x'}, dimensions={0} | all-to-all | bytes 524288 | tf_op jit(solution)/shard_map/all_to_all | solution.py:28
  143.7 29.8 %all_to_all.34 = f32[8,8,512]{2,1,0:T(8,128)S(1)} all-to-all(f32[8,8,512]{2,1,0:T(8,128)S(1)} %broadcast_in_dim.10), channel_id=1, replica_groups=mesh['groups'=2,'z_high'=8,'z_low'=4,'x'=4,'side'=2] {'z_high'}, dimensions={0} | all-to-all | bytes 262144 | tf_op jit(solution)/shard_map/all_to_all | solution.py:28
  173.6 12.4 %all_to_all.35.mine_ref = f32[16,8,512]{2,1,0:T(8,128)S(1)} all-to-all(f32[16,8,512]{2,1,0:T(8,128)S(1)} %broadcast_in_dim.11), channel_id=1, replica_groups=mesh['groups'=2,'z_high'=8,'z_low'=4,'x'=4,'side'=2] {'z_low','x'}, dimensions={0} | all-to-all | bytes 524288 | tf_op jit(solution)/shard_map/all_to_all | solution.py:28
  186.0 0.0 copy-start
  186.0 8.3 %collective-permute-start.3 = (f32[16,8,512]{2,1,0:T(8,128)S(1)}, f32[16,8,512]{2,1,0:T(8,128)S(1)}, u32[]{:S(2)}, u32[]{:S(2)}) collective-permute-start(f32[16,8,512]{2,1,0:T(8,128)S(1)} %all_to_all.35.mine_ref), channel_id=1, source_target_pairs={{0,1},{1,0},{2,3},{3,2},{4,5},{5,4},{6,7},{7,6},{8,9},{9,8},{10,11... | collective-permute-start | bytes 786440 | tf_op jit(solution)/shard_map/ppermute | solution.py:227
  194.2 1.1 collective-permute-done.3.other_ref
  195.4 0.0 copy-start.2
  195.4 0.0 copy-done
  195.4 0.7 copy-done.2
  196.1 12.9 %factor.1 = f32[1,64,512]{2,1,0:T(8,128)} custom-call(s32[1]{0:T(128)} %bitcast.side_ref, f32[16,8,512]{2,1,0:T(8,128)} %copy-done, f32[16,8,512]{2,1,0:T(8,128)} %copy-done.2, f32[64,512]{1,0:T(8,128)} %get-tuple-element.18.rows_ref, bf16[2048,512]{1,0:T(8,128)(2,1)} %get-tuple-element.14.top_ref, bf16[2048,512]{1,0:T(8,128)(2,1)} %get-tuple-element.15.low_ref), custom_call_target="tpu_custom_call" | custom-call | tf_op jit(solution)/shard_map/factor/pallas_call | solution.py:230
  (9 shorter events, 0.2 us)
Async XLA Ops:
  7.1 44.7 %collective-permute-start = (f32[16,8,512]{2,1,0:T(8,128)}, f32[16,8,512]{2,1,0:T(8,128)S(1)}, u32[]{:S(2)}, u32[]{:S(2)}) collective-permute-start(f32[16,8,512]{2,1,0:T(8,128)} %get-tuple-element.12), channel_id=1, source_target_pairs={{1,0},{3,2},{5,4},{7,6},{9,8},{11,10},{13,12},{15,14},{17,16},{19,... | collective-permute-start | bytes 786440 | tf_op jit(solution)/shard_map/ppermute | solution.py:213
  115.6 6.3 %copy-start.1 = (f32[16,8,512]{2,1,0:T(8,128)}, f32[16,8,512]{2,1,0:T(8,128)S(1)}, u32[]{:S(2)}) copy-start(f32[16,8,512]{2,1,0:T(8,128)S(1)} %all_to_all.32.mine_ref) | copy-start | bytes 786436
  115.7 6.3 %collective-permute-start.1 = (f32[16,8,512]{2,1,0:T(8,128)S(1)}, f32[16,8,512]{2,1,0:T(8,128)S(1)}, u32[]{:S(2)}, u32[]{:S(2)}) collective-permute-start(f32[16,8,512]{2,1,0:T(8,128)S(1)} %all_to_all.32.mine_ref), channel_id=1, source_target_pairs={{1,0},{3,2},{5,4},{7,6},{9,8},{11,10},{13,12},{15,14},{17,16},{19,... | collective-permute-start | bytes 786440 | tf_op jit(solution)/shard_map/ppermute | solution.py:215
  122.0 0.7 copy-start.3
  128.0 3.7 %collective-permute-start.2 = (f32[16,8,512]{2,1,0:T(8,128)}, f32[16,8,512]{2,1,0:T(8,128)S(1)}, u32[]{:S(2)}, u32[]{:S(2)}) collective-permute-start(f32[16,8,512]{2,1,0:T(8,128)} %get-tuple-element.17), channel_id=1, source_target_pairs={{0,1},{2,3},{4,5},{6,7},{8,9},{10,11},{12,13},{14,15},{16,17},{18,... | collective-permute-start | bytes 786440 | tf_op jit(solution)/shard_map/ppermute | solution.py:225
  186.0 9.4 %copy-start = (f32[16,8,512]{2,1,0:T(8,128)}, f32[16,8,512]{2,1,0:T(8,128)S(1)}, u32[]{:S(2)}) copy-start(f32[16,8,512]{2,1,0:T(8,128)S(1)} %all_to_all.35.mine_ref) | copy-start | bytes 786436
  186.0 9.4 %collective-permute-start.3 = (f32[16,8,512]{2,1,0:T(8,128)S(1)}, f32[16,8,512]{2,1,0:T(8,128)S(1)}, u32[]{:S(2)}, u32[]{:S(2)}) collective-permute-start(f32[16,8,512]{2,1,0:T(8,128)S(1)} %all_to_all.35.mine_ref), channel_id=1, source_target_pairs={{0,1},{1,0},{2,3},{3,2},{4,5},{5,4},{6,7},{7,6},{8,9},{9,8},{10,11... | collective-permute-start | bytes 786440 | tf_op jit(solution)/shard_map/ppermute | solution.py:227
  195.4 0.7 copy-start.2

commit v3 on v2

--- a/solution.py
+++ b/solution.py
@@ -19,8 +19,9 @@
 F32 = jnp.float32
 BF16 = jnp.bfloat16
 HIGH = lax.Precision.HIGHEST
+ROOM = pltpu.CompilerParams(vmem_limit_bytes=20 * 1024 * 1024)
 VMEM = pl.BlockSpec(memory_space=pltpu.VMEM)
-ANY = pl.BlockSpec(memory_space=pl.ANY)
+HBM = pl.BlockSpec(memory_space=pltpu.HBM)
 SMEM = pl.BlockSpec(memory_space=pltpu.SMEM)
 
 
@@ -36,6 +37,10 @@
     own = jnp.sum(exchanged(blocks, NEAR), axis=0)
     own = jnp.sum(to_all(own, FAR), axis=0)
     return to_all(own, NEAR)
+
+
+def in_hbm(x):
+    return pltpu.with_memory_space_constraint(x, pltpu.HBM)
 
 
 def halves(x):
@@ -73,7 +78,9 @@
     return jnp.concatenate([block_ref[z * X_SIZE + x] for x in range(X_SIZE)], axis=0)
 
 
-def panel_kernel(sketch_ref, data_ref, top_ref, low_ref, send_ref, keep_ref, held, sems):
+def panel_kernel(sketch_in, data_ref, top_ref, low_out, send_ref, keep_ref, sketch_ref, held, low_ref, sems):
+    first_copy = pltpu.make_async_copy(sketch_in, sketch_ref, sems.at[sems.shape[0] - 1])
+    first_copy.start()
     genes, cells = held.shape
     wide = top_ref.shape[0]
     k = sketch_ref.shape[0]
@@ -85,6 +92,7 @@
         copies.append(copy)
     top_ref[genes:] = jnp.zeros((wide - genes, cells), BF16)
     low_ref[genes:] = jnp.zeros((wide - genes, cells), BF16)
+    first_copy.wait()
     stacked = jnp.concatenate(halves(sketch_ref[...]), axis=0)
     for i, first in enumerate(range(0, genes, STEP)):
         rows = min(STEP, genes - first)
@@ -94,6 +102,10 @@
         low_ref[first : first + rows] = low
         value = three(times_t, stacked, top_ref[first : first + STEP], low_ref[first : first + STEP], k)
         put_blocks(send_ref, keep_ref, value, first, False)
+        copies[i] = pltpu.make_async_copy(low_ref.at[pl.ds(first, STEP)], low_out.at[pl.ds(first, STEP)], sems.at[i])
+        copies[i].start()
+    for copy in copies:
+        copy.wait()
 
 
 def lanes(shape):
@@ -104,7 +116,9 @@
     return lax.broadcasted_iota(jnp.int32, shape, 0)
 
 
-def range_kernel(mine_ref, other_ref, top_ref, low_ref, rows_ref, send_ref, keep_ref, panel):
+def range_kernel(mine_ref, other_ref, top_ref, low_in, rows_ref, send_ref, keep_ref, panel, low_ref, sem):
+    fetch = pltpu.make_async_copy(low_in, low_ref, sem)
+    fetch.start()
     k = rows_ref.shape[0]
     half = k // 2
     part = send_ref.shape[2]
@@ -115,7 +129,9 @@
             top, low = halves(whole_rows(ref, z))
             panel[i * half : (i + 1) * half, cols] = top
             panel[k + i * half : k + (i + 1) * half, cols] = low
-    rows = three(times, panel[...], top_ref[...], low_ref[...], k)
+    both = times(panel[...], top_ref[...])
+    fetch.wait()
+    rows = both[:k] + both[k:] + times(panel[:k], low_ref[...])
     rows_ref[...] = rows
     stacked = jnp.concatenate(halves(rows), axis=0)
     padded = jnp.concatenate([rows, jnp.zeros((LANES - k, rows.shape[1]), F32)], axis=0)
@@ -137,6 +153,10 @@
             put_blocks(send_ref, keep_ref, last, wide - LANES, True)
 
 
+def repeated(x, count):
+    return jnp.concatenate([x] * (count // ROWS), axis=0)
+
+
 def factor_inverse(packed, k):
     half = k // 2
     lane, row = lanes((k, LANES)), sublanes((k, LANES))
@@ -148,22 +168,38 @@
     full = jnp.concatenate([square, jnp.zeros((LANES - k, LANES), F32)], axis=0)
     square = jnp.where((lane >= half) & (lane < k) & (row < half), full.T[:k], square)
     work = jnp.where(lane == row + k, 1.0, square)
-    pivots = jnp.ones((k, LANES), F32)
-    for j in range(k):
-        base = j // ROWS * ROWS
-        pivot_row = jnp.broadcast_to(work[j : j + 1], (ROWS, LANES))
-        pivot = jnp.broadcast_to(pivot_row[:, j : j + 1], (ROWS, LANES))
-        scaled = pivot_row / pivot
-        pivots = jnp.where(row == j, jnp.concatenate([pivot] * (k // ROWS), axis=0), pivots)
-        below = work[base:]
-        column = jnp.where(row[base:] > j, jnp.broadcast_to(below[:, j : j + 1], below.shape), 0.0)
-        below = below - column * jnp.concatenate([scaled] * ((k - base) // ROWS), axis=0)
-        work = below if base == 0 else jnp.concatenate([work[:base], below], axis=0)
-    inverse = pltpu.roll(work * lax.rsqrt(pivots), LANES - k, 1)
+    near_row = sublanes((ROWS, LANES))
+    done = []
+    for base in range(0, k, ROWS):
+        count = k - base
+        below = row[:count]
+        block = work[:ROWS]
+        columns = [jnp.broadcast_to(work[:, base + c : base + c + 1], (count, LANES)) for c in range(ROWS)]
+        pivots = jnp.ones((ROWS, LANES), F32)
+        factors, pivot_rows = [], []
+        for c in range(ROWS):
+            pivot = jnp.broadcast_to(columns[c][c : c + 1], (ROWS, LANES))
+            pivots = jnp.where(near_row == c, pivot, pivots)
+            reciprocal = repeated(1.0 / pivot, count)
+            factor = jnp.where(below > c, columns[c] * reciprocal, 0.0)
+            pivot_row = jnp.broadcast_to(block[c : c + 1], (ROWS, LANES))
+            factors.append(factor)
+            pivot_rows.append(pivot_row)
+            for d in range(c + 1, ROWS):
+                columns[d] = columns[d] - factor * jnp.broadcast_to(columns[d][c : c + 1], (count, LANES))
+            block = block - factor[:ROWS] * pivot_row
+        done.append(block * lax.rsqrt(pivots))
+        if count > ROWS:
+            work = work[ROWS:]
+            for factor, pivot_row in zip(factors, pivot_rows):
+                work = work - factor[ROWS:] * repeated(pivot_row, count - ROWS)
+    inverse = pltpu.roll(jnp.concatenate(done, axis=0), LANES - k, 1)
     return jnp.where(lane < k, inverse, 0.0)
 
 
-def factor_kernel(scale, side_ref, mine_ref, other_ref, rows_ref, top_ref, low_ref, out_ref, total, stacked):
+def factor_kernel(scale, side_ref, mine_ref, other_ref, rows_ref, top_ref, low_in, out_ref, total, stacked, low_ref, sem):
+    fetch = pltpu.make_async_copy(low_in, low_ref, sem)
+    fetch.start()
     k = rows_ref.shape[0]
     half = k // 2
     wide = top_ref.shape[0]
@@ -175,6 +211,7 @@
         total[:half, cols] = jnp.where(on_x, mine, other)
         total[half:, cols] = jnp.where(on_x, other, mine)
     inverse = factor_inverse(total[:, wide - LANES :], k)[:, :k]
+    fetch.wait()
 
     @pl.when(on_x)
     def _():
@@ -196,32 +233,38 @@
     k = sketch.shape[0]
     wide = -(-(genes + k * 3 // 4) // (LANES * Z_LOW)) * LANES * Z_LOW
     near_count = Z_LOW * X_SIZE
-    blocks = jax.ShapeDtypeStruct((near_count, ROWS, wide // Z_LOW), F32)
-    parts = jax.ShapeDtypeStruct((wide, cells), BF16)
+    blocks = pltpu.VMEM((near_count, ROWS, wide // Z_LOW), F32)
     on_x = lax.axis_index("side") == 0
     scale = float(cells * lax.axis_size(GROUPS_CELLS[1:])) ** 0.5
     count = -(-genes // STEP)
 
     top, low, send, keep = pl.pallas_call(
         panel_kernel,
-        in_specs=[VMEM, ANY],
-        out_specs=[VMEM] * 4,
-        out_shape=[parts, parts, blocks, blocks],
-        scratch_shapes=[pltpu.VMEM((genes, cells), F32), pltpu.SemaphoreType.DMA((count,))],
+        in_specs=[HBM, HBM],
+        out_specs=[VMEM, HBM, VMEM, VMEM],
+        out_shape=[pltpu.VMEM((wide, cells), BF16), pltpu.HBM((wide, cells), BF16), blocks, blocks],
+        scratch_shapes=[
+            pltpu.VMEM((k, cells), F32),
+            pltpu.VMEM((genes, cells), F32),
+            pltpu.VMEM((wide, cells), BF16),
+            pltpu.SemaphoreType.DMA((count + 1,)),
+        ],
+        compiler_params=ROOM,
         name="panel",
-    )(sketch, datasets)
+    )(in_hbm(sketch), in_hbm(datasets))
     moved = lax.ppermute(send, "side", [(1, 0)])
     mine = sum_over_cells(jnp.where(on_x, moved, keep))
     other = lax.ppermute(mine, "side", [(1, 0)])
 
     rows, send, keep = pl.pallas_call(
         range_kernel,
-        in_specs=[VMEM] * 4,
+        in_specs=[VMEM] * 3 + [HBM],
         out_specs=[VMEM] * 3,
-        out_shape=[jax.ShapeDtypeStruct((k, cells), F32), blocks, blocks],
-        scratch_shapes=[pltpu.VMEM((2 * k, wide), BF16)],
+        out_shape=[pltpu.VMEM((k, cells), F32), blocks, blocks],
+        scratch_shapes=[pltpu.VMEM((2 * k, wide), BF16), pltpu.VMEM((wide, cells), BF16), pltpu.SemaphoreType.DMA],
+        compiler_params=ROOM,
         name="range_rows",
-    )(mine, other, top, low)
+    )(mine, other, top, in_hbm(low))
     moved = lax.ppermute(send, "side", [(0, 1)])
     mine = sum_over_cells(jnp.where(on_x, keep, moved))
     other = lax.ppermute(mine, "side", [(0, 1), (1, 0)])
@@ -229,12 +272,13 @@
     side = lax.axis_index("side").astype(jnp.int32).reshape(1)
     return pl.pallas_call(
         functools.partial(factor_kernel, scale),
-        in_specs=[SMEM] + [VMEM] * 5,
+        in_specs=[SMEM] + [VMEM] * 4 + [HBM],
         out_specs=VMEM,
         out_shape=jax.ShapeDtypeStruct((1, k, cells), F32),
-        scratch_shapes=[pltpu.VMEM((k, wide), F32), pltpu.VMEM((2 * k, wide), BF16)],
+        scratch_shapes=[pltpu.VMEM((k, wide), F32), pltpu.VMEM((2 * k, wide), BF16), pltpu.VMEM((wide, cells), BF16), pltpu.SemaphoreType.DMA],
+        compiler_params=ROOM,
         name="factor",
-    )(side, mine, other, rows, top, low)
+    )(side, mine, other, rows, top, in_hbm(low))
 
 
 def solution(mesh):

time: 209 us -> 195 us (0.933)
  Pallas kernels: 25.3 us -> 13.7 us
    pallas_call x1, Pallas kernels: 12.9 us -> 5.05 us  [per_device(): pl.pallas_call(functools.partial(factor_kernel, scale), in_specs=[SMEM] +...]
    pallas_call x2, Pallas kernels: 12.4 us -> 8.61 us  [the longest x1 5.05 us: per_device(): pl.pallas_call(panel_kernel, in_specs=[HBM, HBM], out_specs=[VMEM, HBM, V...]
    ppermute x1, starting transfers between devices: 8.29 us -> 5.58 us  [per_device(): other = lax.ppermute(mine, 'side', [(0, 1), (1, 0)])]
where the time goes in v3:
time: 195 us
  blocking collectives  118 us (61%)
  starting transfers between devices  57.3 us (29%)
  Pallas kernels  13.7 us (7%)
  waiting for transfers between devices  5.53 us (3%)
    all_to_all x6, blocking collectives, exchanged(): return lax.all_to_all(blocks, axes, 0, 0, tiled=True)  118 us
    ppermute x1, starting transfers between devices, per_device(): moved = lax.ppermute(send, 'side', [(1, 0)])  43.4 us
    ppermute x1, starting transfers between devices, per_device(): other = lax.ppermute(mine, 'side', [(1, 0)])  7.07 us
    ppermute x1, starting transfers between devices, per_device(): other = lax.ppermute(mine, 'side', [(0, 1), (1, 0)])  5.58 us
    pallas_call x1, Pallas kernels, per_device(): pl.pallas_call(functools.partial(factor_kernel, scale), in_specs=[SMEM] +...  5.05 us
    pallas_call x1, Pallas kernels, per_device(): pl.pallas_call(panel_kernel, in_specs=[HBM, HBM], out_specs=[VMEM, HBM, V...  5.05 us
  transfers between devices with their start and end apart: 4, of which 4 were waited for; matrix products, arithmetic and copies ran while one was open for 0% of the time, Pallas kernels for 0%

profile of v3, /device:TPU:33, one launch (start us, length us, event | category | flops | bytes accessed | tf_op | source)
XLA Modules:
  0.0 194.5 jit_solution(11482283458792873793)
XLA Ops:
  0.0 5.1 %panel.1 = (bf16[2048,512]{1,0:T(8,128)(2,1)S(1)}, bf16[2048,512]{1,0:T(8,128)(2,1)}, f32[16,8,512]{2,1,0:T(8,128)S(1)}, f32[16,8,512]{2,1,0:T(8,128)S(1)}) custom-call(f32[64,512]{1,0:T(8,128)} %sketch_in.1, f32[1,2000,512]{2,1,0:T(8,128)} %data_ref.1), custom_call_target="tpu_custom_call" | custom-call | tf_op jit(solution)/shard_map/panel/pallas_call | solution.py:241
  5.1 43.4 %collective-permute-start = (f32[16,8,512]{2,1,0:T(8,128)S(1)}, f32[16,8,512]{2,1,0:T(8,128)S(1)}, u32[]{:S(2)}, u32[]{:S(2)}) collective-permute-start(f32[16,8,512]{2,1,0:T(8,128)S(1)} %get-tuple-element.12), channel_id=1, source_target_pairs={{1,0},{3,2},{5,4},{7,6},{9,8},{11,10},{13,12},{15,14},{17,16},{19,... | collective-permute-start | bytes 786440 | tf_op jit(solution)/shard_map/ppermute | solution.py:255
  48.5 1.1 collective-permute-done
  49.6 12.9 %all_to_all.30 = f32[16,8,512]{2,1,0:T(8,128)S(1)} all-to-all(f32[16,8,512]{2,1,0:T(8,128)S(1)} %broadcast_select_fusion.1), channel_id=1, replica_groups=mesh['groups'=2,'z_high'=8,'z_low'=4,'x'=4,'side'=2] {'z_low','x'}, dimensions={0} | all-to-all | bytes 524288 | tf_op jit(solution)/shard_map/all_to_all | solution.py:29
  62.5 32.1 %all_to_all.31 = f32[8,8,512]{2,1,0:T(8,128)S(1)} all-to-all(f32[8,8,512]{2,1,0:T(8,128)S(1)} %broadcast_in_dim.8), channel_id=1, replica_groups=mesh['groups'=2,'z_high'=8,'z_low'=4,'x'=4,'side'=2] {'z_high'}, dimensions={0} | all-to-all | bytes 262144 | tf_op jit(solution)/shard_map/all_to_all | solution.py:29
  94.7 15.6 %all_to_all.32.mine_ref = f32[16,8,512]{2,1,0:T(8,128)S(1)} all-to-all(f32[16,8,512]{2,1,0:T(8,128)S(1)} %broadcast_in_dim.9), channel_id=1, replica_groups=mesh['groups'=2,'z_high'=8,'z_low'=4,'x'=4,'side'=2] {'z_low','x'}, dimensions={0} | all-to-all | bytes 524288 | tf_op jit(solution)/shard_map/all_to_all | solution.py:29
  110.3 7.1 %collective-permute-start.1 = (f32[16,8,512]{2,1,0:T(8,128)S(1)}, f32[16,8,512]{2,1,0:T(8,128)S(1)}, u32[]{:S(2)}, u32[]{:S(2)}) collective-permute-start(f32[16,8,512]{2,1,0:T(8,128)S(1)} %all_to_all.32.mine_ref), channel_id=1, source_target_pairs={{1,0},{3,2},{5,4},{7,6},{9,8},{11,10},{13,12},{15,14},{17,16},{19,... | collective-permute-start | bytes 786440 | tf_op jit(solution)/shard_map/ppermute | solution.py:257
  117.3 1.1 collective-permute-done.1.other_ref
  118.5 3.6 %range_rows.1 = (f32[64,512]{1,0:T(8,128)S(1)}, f32[16,8,512]{2,1,0:T(8,128)S(1)}, f32[16,8,512]{2,1,0:T(8,128)S(1)}) custom-call(f32[16,8,512]{2,1,0:T(8,128)S(1)} %all_to_all.32.mine_ref, f32[16,8,512]{2,1,0:T(8,128)S(1)} %collective-permute-done.1.other_ref, bf16[2048,512]{1,0:T(8,128)(2,1)S(1)} %get-tuple-element.14.top_ref, ...), custom_call_target="tpu_custom_call" | custom-call | tf_op jit(solution)/shard_map/range_rows/pallas_call | solution.py:259
  122.0 1.3 collective-permute-start.2
  123.3 2.1 %collective-permute-done.2 = f32[16,8,512]{2,1,0:T(8,128)S(1)} collective-permute-done((f32[16,8,512]{2,1,0:T(8,128)S(1)}, f32[16,8,512]{2,1,0:T(8,128)S(1)}, u32[]{:S(2)}, u32[]{:S(2)}) %collective-permute-start.2) | collective-permute-done | bytes 262176 | tf_op jit(solution)/shard_map/ppermute | solution.py:268
  125.5 13.0 %all_to_all.33 = f32[16,8,512]{2,1,0:T(8,128)S(1)} all-to-all(f32[16,8,512]{2,1,0:T(8,128)S(1)} %broadcast_select_fusion), channel_id=1, replica_groups=mesh['groups'=2,'z_high'=8,'z_low'=4,'x'=4,'side'=2] {'z_low','x'}, dimensions={0} | all-to-all | bytes 524288 | tf_op jit(solution)/shard_map/all_to_all | solution.py:29
  138.6 27.6 %all_to_all.34 = f32[8,8,512]{2,1,0:T(8,128)S(1)} all-to-all(f32[8,8,512]{2,1,0:T(8,128)S(1)} %broadcast_in_dim.10), channel_id=1, replica_groups=mesh['groups'=2,'z_high'=8,'z_low'=4,'x'=4,'side'=2] {'z_high'}, dimensions={0} | all-to-all | bytes 262144 | tf_op jit(solution)/shard_map/all_to_all | solution.py:29
  166.2 16.5 %all_to_all.35.mine_ref = f32[16,8,512]{2,1,0:T(8,128)S(1)} all-to-all(f32[16,8,512]{2,1,0:T(8,128)S(1)} %broadcast_in_dim.11), channel_id=1, replica_groups=mesh['groups'=2,'z_high'=8,'z_low'=4,'x'=4,'side'=2] {'z_low','x'}, dimensions={0} | all-to-all | bytes 524288 | tf_op jit(solution)/shard_map/all_to_all | solution.py:29
  182.7 5.6 %collective-permute-start.3 = (f32[16,8,512]{2,1,0:T(8,128)S(1)}, f32[16,8,512]{2,1,0:T(8,128)S(1)}, u32[]{:S(2)}, u32[]{:S(2)}) collective-permute-start(f32[16,8,512]{2,1,0:T(8,128)S(1)} %all_to_all.35.mine_ref), channel_id=1, source_target_pairs={{0,1},{1,0},{2,3},{3,2},{4,5},{5,4},{6,7},{7,6},{8,9},{9,8},{10,11... | collective-permute-start | bytes 786440 | tf_op jit(solution)/shard_map/ppermute | solution.py:270
  188.3 1.1 collective-permute-done.3.other_ref
  189.5 5.1 %factor.1 = f32[1,64,512]{2,1,0:T(8,128)} custom-call(s32[1]{0:T(128)} %bitcast.side_ref, f32[16,8,512]{2,1,0:T(8,128)S(1)} %all_to_all.35.mine_ref, f32[16,8,512]{2,1,0:T(8,128)S(1)} %collective-permute-done.3.other_ref, f32[64,512]{1,0:T(8,128)S(1)} %get-tuple-element.18.rows_ref, bf16[2048,512]{1,0:T(8,128)(2,1)S(1)} %get-tuple-element.14.top_ref, ...), custom_call_target="tpu_custom_call" | custom-call | tf_op jit(solution)/shard_map/factor/pallas_call | solution.py:273
  (10 shorter events, 0.2 us)
Async XLA Ops:
  5.1 44.5 %collective-permute-start = (f32[16,8,512]{2,1,0:T(8,128)S(1)}, f32[16,8,512]{2,1,0:T(8,128)S(1)}, u32[]{:S(2)}, u32[]{:S(2)}) collective-permute-start(f32[16,8,512]{2,1,0:T(8,128)S(1)} %get-tuple-element.12), channel_id=1, source_target_pairs={{1,0},{3,2},{5,4},{7,6},{9,8},{11,10},{13,12},{15,14},{17,16},{19,... | collective-permute-start | bytes 786440 | tf_op jit(solution)/shard_map/ppermute | solution.py:255
  110.3 8.2 %collective-permute-start.1 = (f32[16,8,512]{2,1,0:T(8,128)S(1)}, f32[16,8,512]{2,1,0:T(8,128)S(1)}, u32[]{:S(2)}, u32[]{:S(2)}) collective-permute-start(f32[16,8,512]{2,1,0:T(8,128)S(1)} %all_to_all.32.mine_ref), channel_id=1, source_target_pairs={{1,0},{3,2},{5,4},{7,6},{9,8},{11,10},{13,12},{15,14},{17,16},{19,... | collective-permute-start | bytes 786440 | tf_op jit(solution)/shard_map/ppermute | solution.py:257
  122.0 3.5 %collective-permute-start.2 = (f32[16,8,512]{2,1,0:T(8,128)S(1)}, f32[16,8,512]{2,1,0:T(8,128)S(1)}, u32[]{:S(2)}, u32[]{:S(2)}) collective-permute-start(f32[16,8,512]{2,1,0:T(8,128)S(1)} %get-tuple-element.17), channel_id=1, source_target_pairs={{0,1},{2,3},{4,5},{6,7},{8,9},{10,11},{12,13},{14,15},{16,17},{18,... | collective-permute-start | bytes 786440 | tf_op jit(solution)/shard_map/ppermute | solution.py:268
  182.7 6.7 %collective-permute-start.3 = (f32[16,8,512]{2,1,0:T(8,128)S(1)}, f32[16,8,512]{2,1,0:T(8,128)S(1)}, u32[]{:S(2)}, u32[]{:S(2)}) collective-permute-start(f32[16,8,512]{2,1,0:T(8,128)S(1)} %all_to_all.35.mine_ref), channel_id=1, source_target_pairs={{0,1},{1,0},{2,3},{3,2},{4,5},{5,4},{6,7},{7,6},{8,9},{9,8},{10,11... | collective-permute-start | bytes 786440 | tf_op jit(solution)/shard_map/ppermute | solution.py:270
